TPU v7x, 32 devices: a whole 2x2x4 slice. The times are simulated.
32 devices in a mesh: slab: 8 (over z, x), tile: 4 (over y, core).
Axes of the slice: x: 2, y: 2, z: 4, core: 2. Of those that a mesh axis runs over, the one named last changes fastest.
Arguments:
- tiles: bfloat16 [32, 20, 256, 128], P(('slab', 'tile')), may hold values from -6 to 6
- offsets: int32 [32, 2], replicated, may hold values from -3 to 690, as said below
- fracs: int32 [32, 3], replicated, may hold values from 0 to 15
Outputs:
- joined: bfloat16 [128, 946, 128], P(('slab', 'tile'))
Inputs may be any that keep to these rules, and one draw needn't show every extreme that they name: offsets[g, 0] lies within 1 of (g // 4) * 16 - 2, and offsets[g, 1] within 4 of (g % 4) * 230, clipped to 0 .. 690; some tile reaches each end of the plane shift.
All inputs are finite; a program needn't handle non-finite values.
Results may differ from a plain program's by a relative error of at most 0.0038.
Values may be sent and summed in bfloat16 or wider, within the bound.
A program may use at most 64 MiB of HBM per device.

v0:
```python
import jax
import jax.numpy as jnp
from jax import lax
from jax.sharding import PartitionSpec as P

GROUPZ = 16
MARGIN = 2
JIT = 1
STEPY = 230
RY = 26
RX = 16
QUANT = 16


weight_floor = 0.05


def shifted_2(block, axis, distance):
    devices = range(lax.axis_size(axis))
    route = [(i - distance, i) for i in devices if i - distance in devices]
    return lax.ppermute(block, axis, route)


def rising_at(position, ramp_width):
    rising = 0.5 - 0.5 * jnp.cos(jnp.pi * (position + 1.0) / (ramp_width + 1.0))
    return jnp.where(position < ramp_width, rising, jnp.ones_like(rising))


def ramp_at(index_grid, length, ramp_width):
    position = index_grid.astype(jnp.float32)
    mirrored = (length - 1 - index_grid).astype(jnp.float32)
    return jnp.minimum(rising_at(position, ramp_width), rising_at(mirrored, ramp_width))


def ramp(length, ramp_width):
    return ramp_at(jnp.arange(length, dtype=jnp.int32), length, ramp_width)


def resample(raw_tile, fraction_row):
    volume_field = raw_tile.astype(jnp.float32)
    for direction in range(3):
        fraction = fraction_row[direction].astype(jnp.float32) / QUANT
        extent = volume_field.shape[direction]
        shifted = jnp.concatenate(
            [
                lax.slice_in_dim(volume_field, 1, extent, axis=direction),
                jnp.zeros_like(lax.slice_in_dim(volume_field, 0, 1, axis=direction)),
            ],
            axis=direction,
        )
        volume_field = (1.0 - fraction) * volume_field + fraction * shifted
    return volume_field


def lookup_rows(offsets, tile_ids):
    grid = jnp.arange(offsets.shape[0], dtype=jnp.int32)
    hits = tile_ids[:, None] == grid[None, :]
    return jnp.sum(
        jnp.where(hits[:, :, None], offsets[None, :, :], jnp.zeros_like(offsets)[None, :, :]),
        axis=1,
    )


def take_planes(source, positions, usable):
    planes = jnp.take(source, jnp.clip(positions, 0, source.shape[0] - 1), axis=0)
    return jnp.where(usable[:, :, None, None], planes, jnp.zeros_like(planes))


def shards(tiles, offsets, fracs):
    group_size = lax.axis_size("tile")
    group_total = lax.axis_size("slab")
    slab_index = lax.axis_index("slab")
    owner_index = lax.axis_index("tile")
    depth = tiles.shape[1]
    tile_rows = tiles.shape[2]
    columns = tiles.shape[3]
    per_slab = GROUPZ // group_size
    tile_total = offsets.shape[0]
    self_id = slab_index * group_size + owner_index
    fraction_row = lax.dynamic_index_in_dim(fracs, self_id, 0, keepdims=False)
    corner = lax.dynamic_index_in_dim(offsets, self_id, 0, keepdims=False)
    ramp_z = ramp(depth, 2 * MARGIN)
    ramp_y = ramp(tile_rows, RY)
    ramp_x = ramp(columns, RX)
    weight = ramp_z[:, None, None] * ramp_y[None, :, None] * ramp_x[None, None, :]
    blended = (resample(tiles[0], fraction_row) * weight).astype(jnp.bfloat16)
    owners = jnp.arange(group_size, dtype=jnp.int32)
    planes = jnp.arange(per_slab, dtype=jnp.int32)
    own_z = slab_index * GROUPZ + owners[:, None] * per_slab + planes[None, :]
    every = jnp.ones(own_z.shape, bool)
    own_planes = take_planes(blended, own_z - corner[0], every)
    tile_ranks = jnp.arange(group_size, dtype=jnp.int32)
    margin = MARGIN + JIT
    rim_above = shifted_2(blended[:margin], "slab", -1)
    rim_below = shifted_2(blended[depth - margin :], "slab", 1)
    neighbour_rows = lookup_rows(
        offsets,
        jnp.clip(jnp.stack([self_id - group_size, self_id + group_size]), 0, tile_total - 1),
    )
    below_pos = own_z - (neighbour_rows[0, 0] + depth - margin)
    above_pos = own_z - neighbour_rows[1, 0]
    lower_half = (owners < group_size // 2)[:, None]
    rim_planes = jnp.concatenate([rim_below, rim_above], axis=0)
    rim_pos = jnp.where(lower_half, below_pos, margin + above_pos)
    rim_usable = jnp.where(
        lower_half, (below_pos >= 0) & (below_pos < margin), (above_pos >= 0) & (above_pos < margin)
    )
    extra_planes = take_planes(rim_planes, rim_pos, rim_usable)
    outgoing = jnp.stack([own_planes, extra_planes], axis=1)
    received = lax.all_to_all(outgoing, "tile", split_axis=0, concat_axis=0, tiled=True)
    pieces = jnp.concatenate([received[:, 0], received[:, 1]], axis=0)
    side_group = jnp.where(owner_index < group_size // 2, slab_index - 1, slab_index + 1)
    source_group = jnp.concatenate(
        [
            jnp.full((group_size,), slab_index, jnp.int32),
            jnp.full((group_size,), side_group, jnp.int32),
        ]
    )
    source_rank = jnp.concatenate([tile_ranks, tile_ranks])
    group_valid = (source_group >= 0) & (source_group < group_total)
    source_id = jnp.clip(source_group * group_size + source_rank, 0, tile_total - 1)
    source_rows = lookup_rows(offsets, source_id)
    slab_z = self_id * per_slab + planes
    plane_pos = slab_z[None, :] - source_rows[:, 0:1]
    plane_inside = group_valid[:, None] & (plane_pos >= 0) & (plane_pos < depth)
    weight_z = jnp.where(
        plane_inside, ramp_at(jnp.clip(plane_pos, 0, depth - 1), depth, 2 * MARGIN), 0.0
    )
    volume_rows = (group_size - 1) * STEPY + tile_rows
    row_grid = jnp.arange(volume_rows, dtype=jnp.int32)
    row_pos = row_grid[None, :] - source_rows[:, 1:2]
    row_inside = (row_pos >= 0) & (row_pos < tile_rows)
    weight_y = jnp.where(
        row_inside, ramp_at(jnp.clip(row_pos, 0, tile_rows - 1), tile_rows, RY), 0.0
    )
    piece_count = pieces.shape[0]
    target_rows = jnp.clip(
        source_rows[:, 1:2] + jnp.arange(tile_rows, dtype=jnp.int32)[None, :], 0, volume_rows - 1
    )
    flat_rows = (
        jnp.transpose(pieces, (0, 2, 1, 3))
        .reshape(piece_count * tile_rows, per_slab * columns)
        .astype(jnp.float32)
    )
    placed = jax.ops.segment_sum(flat_rows, target_rows.reshape(-1), num_segments=volume_rows)
    numer = jnp.transpose(placed.reshape(volume_rows, per_slab, columns), (1, 0, 2))
    weight_plane = jnp.einsum("kz,ka->za", weight_z, weight_y, precision=lax.Precision.HIGHEST)
    weight_sum = weight_plane[:, :, None] * ramp_x[None, None, :]
    return (numer / jnp.maximum(weight_sum, weight_floor)).astype(jnp.bfloat16)


def solution(mesh):
    in_specs = (P(("slab", "tile"), None, None, None), P(), P())
    out_specs = P(("slab", "tile"), None, None)
    return jax.shard_map(shards, mesh=mesh, in_specs=in_specs, out_specs=out_specs, check_vma=False)
```

profile of v0, /device:TPU:0, one launch (start us, length us, event | category | flops | bytes accessed | tf_op | source)
XLA Modules:
  0.0 88.8 jit_solution(12471675859911475062)
XLA Ops:
  0.0 0.1 fusion.102
  0.1 0.1 fusion.89
  0.1 0.1 fusion.107
  0.2 0.5 copy-done
  0.7 0.1 constant_dynamic-slice_fusion
  0.8 0.5 fusion.134
  1.8 1.6 %convert_element_type.92 = f32[1,20,256,128]{3,2,1,0:T(8,128)S(1)} convert(bf16[1,20,256,128]{3,2,1,0:T(8,128)(2,1)} %param.3) | non-fusion elementwise | flops 655360 | bytes 3932160 | tf_op jit(solution)/shard_map/convert_element_type | solution.py:40
  3.4 0.2 slice_bitcast_fusion
  3.6 1.8 %bitcast_add_fusion = f32[20,256,128]{2,1,0:T(8,128)S(1)} fusion(f32[19,256,128]{2,1,0:T(8,128)S(1)} %slice_bitcast_fusion, f32[]{:T(128)} %bitcast.4, f32[]{:T(128)S(6)} %sub.213, bf16[1,20,256,128]{3,2,1,0:T(8,128)(2,1)} %param.3), kind=kLoop, calls=%fused_computation.7 | loop fusion | flops 2621440 | bytes 6422536 | tf_op jit(solution)/shard_map/add | solution.py:51
  5.5 0.0 copy-start.1
  5.5 2.0 %slice.74 = f32[20,255,128]{2,1,0:T(8,128)} slice(f32[20,256,128]{2,1,0:T(8,128)S(1)} %bitcast_add_fusion), slice={[0:20], [1:256], [0:128]} | slice | bytes 5222400 | tf_op jit(solution)/shard_map/slice | solution.py:46
  7.5 0.3 copy-done.1
  8.4 2.9 %multiply_add_fusion = f32[20,256,128]{2,1,0:T(8,128)S(1)} fusion(f32[20,255,128]{2,1,0:T(8,128)} %slice.74, f32[20,256,128]{2,1,0:T(8,128)} %copy-done.1, f32[]{:T(128)} %bitcast.3, f32[]{:T(128)S(6)} %sub.212), kind=kLoop, calls=%fused_computation.9 | loop fusion | flops 1966080 | bytes 7854088 | tf_op jit(solution)/shard_map/add | solution.py:51
  11.3 2.3 %slice.75 = f32[20,256,127]{2,1,0:T(8,128)} slice(f32[20,256,128]{2,1,0:T(8,128)S(1)} %multiply_add_fusion), slice={[0:20], [0:256], [1:128]} | slice | bytes 5201920 | tf_op jit(solution)/shard_map/slice | solution.py:46
  14.2 0.1 broadcast_multiply_fusion
  14.3 2.3 %multiply_convert_fusion = bf16[20,256,128]{2,1,0:T(8,128)(2,1)S(1)} fusion(f32[20,256,127]{2,1,0:T(8,128)} %slice.75, f32[20,256,128]{2,1,0:T(8,128)S(1)} %multiply_add_fusion, f32[128]{0:T(128)S(1)} %fusion.102, f32[20,256]{1,0:T(8,128)S(1)} %broadcast_multiply_fusion, f32[]{:T(128)} %bitcast.2, f32[]{:T(128)S(6)} %sub.211), kind=kLoop, calls=%fused_computation.8 | loop fusion | flops 3932160 | bytes 6554120 | tf_op jit(solution)/shard_map/convert_element_type | solution.py:86
  16.6 1.1 %copy-done.2 = bf16[20,256,128]{2,1,0:T(8,128)(2,1)} copy-done((bf16[20,256,128]{2,1,0:T(8,128)(2,1)}, bf16[20,256,128]{2,1,0:T(8,128)(2,1)S(1)}, u32[]{:S(2)}) %copy-start.2) | copy-done | bytes 1310744
  17.7 4.9 %collective-permute-start = (bf16[3,256,128]{2,1,0:T(8,128)(2,1)S(1)}, bf16[3,256,128]{2,1,0:T(8,128)(2,1)S(1)}, u32[]{:S(2)}, u32[]{:S(2)}) collective-permute-start(bf16[3,256,128]{2,1,0:T(8,128)(2,1)S(1)} %get-tuple-element.7), channel_id=1, source_target_pairs={{0,4},{4,8},{8,12},{12,16},{16,20},{20,24},{24,28},{1,5},{5,9},{9,... | collective-permute-start | bytes 589832 | tf_op jit(solution)/shard_map/ppermute | solution.py:21
  22.6 1.3 %collective-permute-start.1 = (bf16[3,256,128]{2,1,0:T(8,128)(2,1)S(1)}, bf16[3,256,128]{2,1,0:T(8,128)(2,1)S(1)}, u32[]{:S(2)}, u32[]{:S(2)}) collective-permute-start(bf16[3,256,128]{2,1,0:T(8,128)(2,1)S(1)} %get-tuple-element.8), channel_id=1, source_target_pairs={{4,0},{8,4},{12,8},{16,12},{20,16},{24,20},{28,24},{5,1},{9,5},{13... | collective-permute-start | bytes 589832 | tf_op jit(solution)/shard_map/ppermute | solution.py:21
  23.9 0.1 constant_dynamic-slice_fusion.1
  24.0 0.5 slice.54
  24.5 0.1 add_clamp_fusion
  24.6 0.1 iota_compare_fusion.1
  24.7 0.1 select_reduce_fusion.1
  24.8 0.5 fusion.135
  26.0 1.4 %compare_select_fusion.2 = (s32[4,4,1]{1,0,2:T(4,128)S(1)}, s32[4,4,1]{1,0,2:T(4,128)S(1)}) fusion(s32[]{:T(128)} %bitcast.1, s32[4]{0:T(128)S(1)} %multiply_add_fusion.1, s32[]{:T(128)} %bitcast.11, s32[]{:T(128)} %bitcast.10, pred[4]{0:T(512)(128)(4,1)S(1)} %iota_compare_fusion.2), kind=kLoop, calls=%fused_computation.62 | loop fusion | flops 224 | bytes 160 | tf_op jit(solution)/shard_map/jit(_take)/jit(_where)/select_n | solution.py:65
  27.4 0.1 reshape.463
  27.5 0.1 reshape.455
  27.5 2.1 %gather_fusion = bf16[16,256,128]{2,1,0:T(8,128)(2,1)S(1)} fusion(bf16[20,256,128]{2,1,0:T(8,128)(2,1)} %copy-done.2, s32[1024]{0:T(1024)S(1)} %pad_clamp_fusion.1), kind=kCustom, calls=%fused_computation | custom fusion | bytes 2097216 | tf_op jit(solution)/shard_map/jit(_take)/gather | solution.py:65
  29.6 1.4 %fusion.81 = (pred[4,4]{1,0:T(4,128)(4,1)S(1)}, pred[4,4]{1,0:T(4,128)(4,1)S(1)}, pred[4,4]{1,0:T(4,128)(4,1)S(1)}) fusion(s32[]{:T(128)} %bitcast.11, s32[]{:T(128)} %bitcast.10, s32[4]{0:T(128)S(1)} %multiply_add_fusion.1, pred[4]{0:T(512)(128)(4,1)S(1)} %iota_compare_fusion.2, s32[]{:T(128)} %bitcast.1), kind=kLoop, calls=%fused_computation.108 | loop fusion | flops 432 | bytes 80 | tf_op jit(solution)/shard_map/jit(_where)/select_n | solution.py:105
  31.0 0.0 collective-permute-done
  31.0 0.0 collective-permute-done.1
  31.1 0.7 gather_fusion.1
  31.8 0.3 select_select_fusion
  32.1 1.5 %pad_maximum_fusion = bf16[4,2,4,256,128]{4,3,2,1,0:T(8,128)(2,1)} fusion(bf16[4,1,4,256,128]{4,3,2,1,0:T(8,128)(2,1)S(1)} %get-tuple-element.21, bf16[4,1,4,256,128]{4,3,2,1,0:T(8,128)(2,1)S(1)} %get-tuple-element.22), kind=kLoop, calls=%fused_computation.11 | loop fusion | flops 1048576 | bytes 4194304 | tf_op jit(solution)/shard_map/stack | solution.py:109
  33.7 3.6 %all-to-all-start = ((bf16[4,2,4,256,128]{4,3,2,1,0:T(8,128)(2,1)}), bf16[4,2,4,256,128]{4,3,2,1,0:T(8,128)(2,1)S(1)}, u32[]{:S(2)}, u32[]{:S(2)}) async-start(bf16[4,2,4,256,128]{4,3,2,1,0:T(8,128)(2,1)} %pad_maximum_fusion), calls=%async_computation | async-start | bytes 4194304 | tf_op jit(solution)/shard_map/all_to_all | solution.py:110
  37.3 0.1 fusion.120
  37.4 0.1 iota_compare_fusion
  37.5 0.1 select_reduce_fusion
  37.6 0.1 clamp_bitcast_fusion
  37.7 1.1 %fusion.5 = f32[4,946]{0,1:T(8,128)S(1)} fusion(s32[8]{0:T(128)S(1)} %get-tuple-element.13, s32[8]{0:T(128)S(1)} %get-tuple-element.12, s32[4]{0:T(128)S(1)} %iota_add_fusion.2, pred[8]{0:T(512)(128)(4,1)S(1)} %compare_and_fusion), kind=kOutput, calls=%fused_computation.20 | convolution fusion | flops 530496 | bytes 15224 | tf_op jit(solution)/shard_map/kz,ka->za/dot_general | solution.py:147
  38.9 24.0 %all-to-all-done = bf16[4,2,4,256,128]{4,3,2,1,0:T(8,128)(2,1)S(1)} async-done(((bf16[4,2,4,256,128]{4,3,2,1,0:T(8,128)(2,1)}), bf16[4,2,4,256,128]{4,3,2,1,0:T(8,128)(2,1)S(1)}, u32[]{:S(2)}, u32[]{:S(2)}) %all-to-all-start) | async-done | bytes 2097184 | tf_op jit(solution)/shard_map/all_to_all | solution.py:110
  62.9 0.1 slice_bitcast_fusion.2
  63.0 0.3 convert_bitcast_fusion
  63.3 4.6 %copy.28 = f32[8,256,4,128]{3,2,1,0:T(4,128)} copy(f32[8,256,4,128]{3,1,2,0:T(8,128)S(1)} %convert_bitcast_fusion) | data formatting | bytes 8388608 | tf_op jit(solution)/shard_map/convert_element_type | solution.py:143
  68.0 14.8 %scatter_custom_fusion = f32[946,512]{1,0:T(8,128)S(1)} fusion(s32[2048]{0:T(1024)S(1)} %bitcast.45, f32[256,8,4,128]{3,2,1,0:T(4,128)} %bitcast.42, f32[]{:T(128)} %constant.50.clone.1), kind=kCustom, calls=%fused_computation.3 | custom fusion | flops 1048576 | bytes 6131716 | tf_op jit(solution)/shard_map/scatter-add | solution.py:145
  82.7 1.9 %reshape.451 = f32[946,4,128]{2,1,0:T(4,128)} reshape(f32[946,512]{1,0:T(8,128)S(1)} %scatter_custom_fusion) | data formatting | bytes 3874816 | tf_op jit(solution)/shard_map/reshape | solution.py:146
  84.7 4.1 %fusion.3 = bf16[4,946,128]{2,0,1:T(4,128)(2,1)} fusion(f32[946,4,128]{2,1,0:T(4,128)} %reshape.451, f32[128]{0:T(128)S(1)} %fusion.102, f32[4,946]{0,1:T(8,128)S(1)} %fusion.5), kind=kLoop, calls=%fused_computation.13 | loop fusion | flops 1937408 | bytes 2921760 | tf_op jit(solution)/shard_map/convert_element_type | solution.py:149
  (16 shorter events, 0.1 us)
Async XLA Ops:
  0.0 0.7 copy-start
  5.5 2.4 %copy-start.1 = (f32[20,256,128]{2,1,0:T(8,128)}, f32[20,256,128]{2,1,0:T(8,128)S(1)}, u32[]{:S(2)}) copy-start(f32[20,256,128]{2,1,0:T(8,128)S(1)} %bitcast_add_fusion) | copy-start | bytes 7864324
  14.3 9.7 %copy-start.3 = (s32[32,2]{0,1:T(2,128)S(1)}, s32[32,2]{0,1:T(2,128)}, u32[]{:S(2)}) copy-start(s32[32,2]{0,1:T(2,128)} %param.4) | copy-start | bytes 772
  16.6 1.1 %copy-start.2 = (bf16[20,256,128]{2,1,0:T(8,128)(2,1)}, bf16[20,256,128]{2,1,0:T(8,128)(2,1)S(1)}, u32[]{:S(2)}) copy-start(bf16[20,256,128]{2,1,0:T(8,128)(2,1)S(1)} %multiply_convert_fusion) | copy-start | bytes 3932164
  17.7 13.3 %collective-permute-start = (bf16[3,256,128]{2,1,0:T(8,128)(2,1)S(1)}, bf16[3,256,128]{2,1,0:T(8,128)(2,1)S(1)}, u32[]{:S(2)}, u32[]{:S(2)}) collective-permute-start(bf16[3,256,128]{2,1,0:T(8,128)(2,1)S(1)} %get-tuple-element.7), channel_id=1, source_target_pairs={{0,4},{4,8},{8,12},{12,16},{16,20},{20,24},{24,28},{1,5},{5,9},{9,... | collective-permute-start | bytes 589832 | tf_op jit(solution)/shard_map/ppermute | solution.py:21
  22.6 8.4 %collective-permute-start.1 = (bf16[3,256,128]{2,1,0:T(8,128)(2,1)S(1)}, bf16[3,256,128]{2,1,0:T(8,128)(2,1)S(1)}, u32[]{:S(2)}, u32[]{:S(2)}) collective-permute-start(bf16[3,256,128]{2,1,0:T(8,128)(2,1)S(1)} %get-tuple-element.8), channel_id=1, source_target_pairs={{4,0},{8,4},{12,8},{16,12},{20,16},{24,20},{28,24},{5,1},{9,5},{13... | collective-permute-start | bytes 589832 | tf_op jit(solution)/shard_map/ppermute | solution.py:21
  33.7 29.2 %all-to-all-start = ((bf16[4,2,4,256,128]{4,3,2,1,0:T(8,128)(2,1)}), bf16[4,2,4,256,128]{4,3,2,1,0:T(8,128)(2,1)S(1)}, u32[]{:S(2)}, u32[]{:S(2)}) async-start(bf16[4,2,4,256,128]{4,3,2,1,0:T(8,128)(2,1)} %pad_maximum_fusion), calls=%async_computation | async-start | bytes 4194304 | tf_op jit(solution)/shard_map/all_to_all | solution.py:110
where the time goes:
time: 89.9 us; the launch traced here: 88.8 us
  other arithmetic  33.4 us (37%)
  waiting for transfers between devices  24 us (27%)
  local copies, waits for them, and re-layouts  17.8 us (20%)
  starting transfers between devices  9.78 us (11%)
  between operations  2.68 us (3%)
  matrix products  1.13 us (1%)
    all_to_all x1, waiting for transfers between devices, shards(): lax.all_to_all(outgoing, 'tile', split_axis=0, concat_axis=0, tiled=True)  24 us
    scatter-add x1, other arithmetic, shards(): jax.ops.segment_sum(flat_rows, target_rows.reshape(-1), num_segments=volu...  14.8 us
    ppermute x2, starting transfers between devices, shifted_2(): return lax.ppermute(block, axis, route)  6.17 us
    add x2, other arithmetic, resample(): volume_field = (1.0 - fraction) * volume_field + fraction * shifted  4.7 us
    convert_element_type x1, local copies, waits for them, and re-layouts, shards(): flat_rows = jnp.transpose(pieces, (0, 2, 1, 3)).reshape(piece_count * til...  4.64 us
    slice x3, local copies, waits for them, and re-layouts, resample(): lax.slice_in_dim(volume_field, 1, extent, axis=direction)  4.43 us
    convert_element_type x1, other arithmetic, shards(): return (numer / jnp.maximum(weight_sum, weight_floor)).astype(jnp.bfloat16)  4.14 us
    all_to_all x1, starting transfers between devices, shards(): lax.all_to_all(outgoing, 'tile', split_axis=0, concat_axis=0, tiled=True)  3.61 us
  transfers between devices with their start and end apart: 3, of which 1 were waited for; matrix products, arithmetic and copies ran while one was open for 9% of the time, Pallas kernels for 0%

commit v1 on v0

v1 whole, which is shorter than its diff:
```python
import functools

import jax
import jax.numpy as jnp
import numpy as np
from jax import lax
from jax.experimental import pallas as pl
from jax.experimental.pallas import tpu as pltpu
from jax.sharding import PartitionSpec as P

GROUPZ = 16
MARGIN = 2
JIT = 1
STEPY = 230
JITY = 4
RY = 26
RX = 16
QUANT = 16
EDGE = MARGIN + JIT
PADY = 16
PADZ = 24

weight_floor = 0.05
MESH = pl.DeviceIdType.MESH


def ramp(length, ramp_width):
    position = np.arange(length, dtype=np.float64)
    rising = 0.5 - 0.5 * np.cos(np.pi * (position + 1.0) / (ramp_width + 1.0))
    rising = np.where(position < ramp_width, rising, 1.0)
    return np.minimum(rising, rising[::-1])


def frame_start(rank):
    if isinstance(rank, int):
        return max((rank * STEPY - JITY) // 8 * 8, 0)
    return jnp.maximum((rank * STEPY + 8 - JITY) // 8 * 8 - 8, 0)


def round_up(value, step):
    return -(-value // step) * step


def kernel(
    groups, n, per, depth, tile_rows, frame, acc_rows,
    offs, fracs, rampz, table, tile_ref, out_ref,
    raw, coef, wa, wb, blend, edge_send, edge_recv, recv, acc, rec,
    load_sem, es_sem, er_sem, s_sem, r_sem,
):
    g = lax.axis_index("slab")
    r = lax.axis_index("tile")
    me = g * n + r
    low = r < n // 2
    cols = raw.shape[2]
    last = n - 1

    load = pltpu.make_async_copy(tile_ref.at[0], raw.at[pl.ds(0, depth)], load_sem)
    load.start()

    barrier = pltpu.get_barrier_semaphore()
    for i in range(1, n):
        pl.semaphore_signal(
            barrier, inc=1, device_id=(g, lax.rem(r + i, n)), device_id_type=MESH
        )
    has_below = g > 0
    has_above = g < groups - 1

    @pl.when(has_below)
    def _():
        pl.semaphore_signal(barrier, inc=1, device_id=(g - 1, r), device_id_type=MESH)

    @pl.when(has_above)
    def _():
        pl.semaphore_signal(barrier, inc=1, device_id=(g + 1, r), device_id_type=MESH)

    def table_row(at):
        return jnp.clip(at, 0, table.shape[0] - frame)

    def rampz_at(z):
        return rampz[jnp.clip(z + PADZ, 0, rampz.shape[0] - 1)]

    corner = offs[0, me]
    shift = offs[1, me] - frame_start(r)
    fz = fracs[0, me].astype(jnp.float32) / QUANT
    fy = fracs[1, me].astype(jnp.float32) / QUANT
    fx = fracs[2, me].astype(jnp.float32) / QUANT
    row = lax.broadcasted_iota(jnp.int32, (frame, tile_rows), 0)
    col = lax.broadcasted_iota(jnp.int32, (frame, tile_rows), 1)
    behind = col - row + shift
    lerp_y = jnp.where(behind == 0, 1.0 - fy, jnp.where(behind == 1, fy, 0.0))
    coef[:, :tile_rows] = ((1.0 - fz) * lerp_y).astype(jnp.bfloat16)
    coef[:, tile_rows:] = (fz * lerp_y).astype(jnp.bfloat16)
    weight = table[pl.ds(table_row(PADY - shift), frame), :]
    lane = lax.broadcasted_iota(jnp.int32, (frame, cols), 1)
    wa[...] = weight * (1.0 - fx)
    wb[...] = jnp.where(lane < cols - 1, weight * fx, 0.0)
    raw[depth] = jnp.zeros(raw.shape[1:], raw.dtype)

    def planes(store, first, count):
        at = [jnp.clip(first + j, 0, depth - 1) for j in range(count)]
        top = jnp.concatenate([raw[z] for z in at], axis=1)
        bottom = jnp.concatenate([raw[z + 1] for z in at], axis=1)
        mixed = jnp.dot(
            coef[...], jnp.concatenate([top, bottom], axis=0),
            preferred_element_type=jnp.float32,
        )
        for j in range(count):
            part = mixed[:, j * cols : (j + 1) * cols]
            value = part * wa[...] + pltpu.roll(part, cols - 1, 1) * wb[...]
            store(j, (value * rampz_at(first + j)).astype(jnp.bfloat16))

    base = g * GROUPZ - corner

    def mirrored(owner):
        return jnp.where(low, owner, last - owner)

    def blend_owner(owner):
        def store(j, value):
            blend[owner, j] = value

        planes(store, base + owner * per, per)

    def send_owner(owner):
        @pl.when(owner != r)
        def _():
            pltpu.make_async_remote_copy(
                src_ref=blend.at[owner], dst_ref=recv.at[r],
                send_sem=s_sem.at[owner], recv_sem=r_sem.at[r],
                device_id=(g, owner), device_id_type=MESH,
            ).start()

    def edge_copy(side):
        return pltpu.make_async_remote_copy(
            src_ref=edge_send.at[side], dst_ref=edge_recv.at[side],
            send_sem=es_sem.at[side], recv_sem=er_sem.at[side],
            device_id=(g + 1 - 2 * side, r), device_id_type=MESH,
        )

    def sends_to(side):
        return jnp.where(side == 0, g < groups - 1, g > 0)

    def gets_from(side):
        return jnp.where(side == 0, g > 0, g < groups - 1)

    def send_edge(side):
        def store(j, value):
            edge_send[side, j] = value

        planes(store, base + jnp.where(side == 0, GROUPZ, -EDGE), EDGE)

        @pl.when(sends_to(side))
        def _():
            edge_copy(side).start()

    edge_planes = list(range(EDGE)) + list(range(GROUPZ - EDGE, GROUPZ))
    bound = sorted({q // per for q in edge_planes}, reverse=True)
    free = [o for o in range(last, -1, -1) if o not in bound]
    far_side = jnp.where(low, 1, 0)

    load.wait()
    pl.semaphore_wait(barrier, n - 1 + jnp.where(has_below, 1, 0) + jnp.where(has_above, 1, 0))
    send_edge(far_side)
    for o in free[: len(free) // 2]:
        blend_owner(mirrored(o))
        send_owner(mirrored(o))
    send_edge(1 - far_side)
    for o in free[len(free) // 2 :]:
        blend_owner(mirrored(o))
        send_owner(mirrored(o))
    for o in bound:
        blend_owner(mirrored(o))

    for step in range(2):
        side = far_side if step == 0 else 1 - far_side

        @pl.when(gets_from(side))
        def _():
            edge_copy(side).wait_recv()
            for p in range(EDGE):
                q = p + jnp.where(side == 0, 0, GROUPZ - EDGE)
                owner, j = q // per, q % per
                blend[owner, j] = (
                    blend[owner, j].astype(jnp.float32)
                    + edge_recv[side, p].astype(jnp.float32)
                ).astype(jnp.bfloat16)

        for o in bound:
            if (o >= n // 2) == (step == 0):
                send_owner(mirrored(o))

    rec[...] = jnp.zeros_like(rec)
    for k in range(n):
        s = frame_start(k)
        totals = [0.0] * per
        for delta in (-1, 0, 1):
            group = jnp.clip(g + delta, 0, groups - 1)
            exists = jnp.where(group == g + delta, 1.0, 0.0)
            z0 = offs[0, group * n + k]
            wy = table[pl.ds(table_row(PADY + s - offs[1, group * n + k]), frame), :]
            for j in range(per):
                z = g * GROUPZ + r * per + j - z0
                totals[j] = totals[j] + wy * (rampz_at(z) * exists)
        for j in range(per):
            rec[j, s : s + frame] = rec[j, s : s + frame] + totals[j]
    rec[...] = 1.0 / jnp.maximum(rec[...], weight_floor)

    acc[...] = jnp.zeros_like(acc)

    def add(k, source):
        s = pl.multiple_of(frame_start(k), 8)
        for j in range(per):
            acc[j, pl.ds(s, frame)] = acc[j, pl.ds(s, frame)] + source[j].astype(jnp.float32)

    add(r, blend.at[r])
    for i in range(1, n):
        k = ((r // 2 + i // 2) % (n // 2)) * 2 + (r + i) % 2
        pltpu.make_async_remote_copy(
            src_ref=blend.at[r], dst_ref=recv.at[k],
            send_sem=s_sem.at[k], recv_sem=r_sem.at[k],
            device_id=(g, k), device_id_type=MESH,
        ).wait_recv()
        add(k, recv.at[k])
    rows = out_ref.shape[1]
    for j in range(per):
        out_ref[j] = (acc[j, :rows] * rec[j, :rows]).astype(jnp.bfloat16)

    for i in range(1, n):
        k = lax.rem(r + i, n)
        pltpu.make_async_remote_copy(
            src_ref=blend.at[k], dst_ref=recv.at[r],
            send_sem=s_sem.at[k], recv_sem=r_sem.at[r],
            device_id=(g, k), device_id_type=MESH,
        ).wait_send()
    for side in range(2):
        @pl.when(sends_to(side))
        def _():
            edge_copy(side).wait_send()


def solution(mesh):
    groups, n = mesh.shape["slab"], mesh.shape["tile"]

    def shards(tiles, offsets, fracs):
        _, depth, tile_rows, cols = tiles.shape
        per = GROUPZ // n
        rows = (n - 1) * STEPY + tile_rows
        reach = max(
            min(k * STEPY + JITY, rows - tile_rows) + tile_rows - frame_start(k) for k in range(n)
        )
        frame = round_up(reach, 16)
        acc_rows = round_up(max(rows, frame_start(n - 1) + frame), 16)
        plane = ramp(tile_rows, RY)[:, None] * ramp(cols, RX)[None, :]
        table = np.zeros((round_up(PADY + frame + 8, 8), cols), np.float32)
        table[PADY : PADY + tile_rows] = plane
        rampz = np.zeros((depth + 2 * PADZ,), np.float32)
        rampz[PADZ : PADZ + depth] = ramp(depth, 2 * MARGIN)
        bf16, f32 = jnp.bfloat16, jnp.float32
        dma = pltpu.SemaphoreType.DMA
        return pl.pallas_call(
            functools.partial(kernel, groups, n, per, depth, tile_rows, frame, acc_rows),
            out_shape=jax.ShapeDtypeStruct((per, rows, cols), bf16),
            in_specs=[pl.BlockSpec(memory_space=pltpu.SMEM)] * 3
            + [pl.BlockSpec(memory_space=pltpu.VMEM), pl.BlockSpec(memory_space=pl.ANY)],
            out_specs=pl.BlockSpec(memory_space=pltpu.VMEM),
            scratch_shapes=[
                pltpu.VMEM((depth + 1, tile_rows, cols), bf16),
                pltpu.VMEM((frame, 2 * tile_rows), bf16),
                pltpu.VMEM((frame, cols), f32),
                pltpu.VMEM((frame, cols), f32),
                pltpu.VMEM((n, per, frame, cols), bf16),
                pltpu.VMEM((2, EDGE, frame, cols), bf16),
                pltpu.VMEM((2, EDGE, frame, cols), bf16),
                pltpu.VMEM((n, per, frame, cols), bf16),
                pltpu.VMEM((per, acc_rows, cols), f32),
                pltpu.VMEM((per, acc_rows, cols), f32),
                dma, dma((2,)), dma((2,)), dma((n,)), dma((n,)),
            ],
            compiler_params=pltpu.CompilerParams(collective_id=0, has_side_effects=True),
        )(offsets.T, fracs.T, jnp.asarray(rampz), jnp.asarray(table), tiles)

    in_specs = (P(("slab", "tile"), None, None, None), P(), P())
    out_specs = P(("slab", "tile"), None, None)
    return jax.shard_map(shards, mesh=mesh, in_specs=in_specs, out_specs=out_specs, check_vma=False)
```

time: 89.9 us -> 25.3 us (0.28)
  the two profiles are of different devices: /device:TPU:0 before, /device:TPU:29 now
where the time goes in v1:
time: 25.3 us; the launch traced here: 25.1 us
  Pallas kernels  22.5 us (89%)
  local copies, waits for them, and re-layouts  2.51 us (10%)
    pallas_call x1, Pallas kernels, shards(): pl.pallas_call(functools.partial(kernel, groups, n, per, depth, tile_rows...  22.5 us
    pallas_call x1, local copies, waits for them, and re-layouts, shards(): pl.pallas_call(functools.partial(kernel, groups, n, per, depth, tile_rows...  2.51 us

profile of v1, /device:TPU:29, one launch (start us, length us, event | category | flops | bytes accessed | tf_op | source)
XLA Modules:
  0.0 25.1 jit_solution(13850614881898033755)
XLA Ops:
  0.0 22.5 %shard_map.55 = bf16[4,946,128]{2,1,0:T(8,128)(2,1)} custom-call(s32[2,32]{1,0:T(2,128)} %bitcast.3, s32[3,32]{1,0:T(4,128)} %bitcast.2, f32[68]{0:T(128)} %constant.4.clone.rampz, f32[296,128]{1,0:T(8,128)} %constant.5.clone.table, bf16[1,20,256,128]{3,2,1,0:T(8,128)(2,1)} %tile_ref.1), custom_call_target="tpu_custom_call" | custom-call | tf_op jit(solution)/shard_map/pallas_call | solution.py:259
  22.5 2.5 %copy.6 = bf16[4,946,128]{2,0,1:T(4,128)(2,1)} copy(bf16[4,946,128]{2,1,0:T(8,128)(2,1)} %shard_map.55) | data formatting | bytes 1937408 | tf_op jit(solution)/shard_map/pallas_call | solution.py:259

commit v2 on v1

--- a/solution.py
+++ b/solution.py
@@ -129,6 +129,31 @@
                 device_id=(g, owner), device_id_type=MESH,
             ).start()
 
+    def send_part(owner, first, count):
+        if count:
+            @pl.when(owner != r)
+            def _():
+                part = pl.ds(first, count)
+                pltpu.make_async_remote_copy(
+                    src_ref=blend.at[owner, part], dst_ref=recv.at[r, part],
+                    send_sem=s_sem.at[owner], recv_sem=r_sem.at[r],
+                    device_id=(g, owner), device_id_type=MESH,
+                ).start()
+
+    def edge_count(o):
+        o = max(o, last - o)
+        return sum(1 for j in range(per) if o * per + j >= GROUPZ - EDGE)
+
+    def send_inner(o):
+        e = edge_count(o)
+        upper = low if o >= n // 2 else jnp.logical_not(low)
+        send_part(mirrored(o), jnp.where(upper, 0, e), per - e)
+
+    def send_bound(o):
+        e = edge_count(o)
+        upper = low if o >= n // 2 else jnp.logical_not(low)
+        send_part(mirrored(o), jnp.where(upper, per - e, 0), e)
+
     def edge_copy(side):
         return pltpu.make_async_remote_copy(
             src_ref=edge_send.at[side], dst_ref=edge_recv.at[side],
@@ -142,40 +167,20 @@
     def gets_from(side):
         return jnp.where(side == 0, g > 0, g < groups - 1)
 
-    def send_edge(side):
+    def blend_edge(side):
         def store(j, value):
             edge_send[side, j] = value
 
         planes(store, base + jnp.where(side == 0, GROUPZ, -EDGE), EDGE)
 
+    def send_edge(side):
         @pl.when(sends_to(side))
         def _():
             edge_copy(side).start()
 
-    edge_planes = list(range(EDGE)) + list(range(GROUPZ - EDGE, GROUPZ))
-    bound = sorted({q // per for q in edge_planes}, reverse=True)
-    free = [o for o in range(last, -1, -1) if o not in bound]
-    far_side = jnp.where(low, 1, 0)
-
-    load.wait()
-    pl.semaphore_wait(barrier, n - 1 + jnp.where(has_below, 1, 0) + jnp.where(has_above, 1, 0))
-    send_edge(far_side)
-    for o in free[: len(free) // 2]:
-        blend_owner(mirrored(o))
-        send_owner(mirrored(o))
-    send_edge(1 - far_side)
-    for o in free[len(free) // 2 :]:
-        blend_owner(mirrored(o))
-        send_owner(mirrored(o))
-    for o in bound:
-        blend_owner(mirrored(o))
-
-    for step in range(2):
-        side = far_side if step == 0 else 1 - far_side
-
+    def add_edge(side):
         @pl.when(gets_from(side))
         def _():
-            edge_copy(side).wait_recv()
             for p in range(EDGE):
                 q = p + jnp.where(side == 0, 0, GROUPZ - EDGE)
                 owner, j = q // per, q % per
@@ -184,9 +189,39 @@
                     + edge_recv[side, p].astype(jnp.float32)
                 ).astype(jnp.bfloat16)
 
-        for o in bound:
-            if (o >= n // 2) == (step == 0):
-                send_owner(mirrored(o))
+    def wait_edge(side):
+        @pl.when(gets_from(side))
+        def _():
+            edge_copy(side).wait_recv()
+
+    edge_planes = list(range(EDGE)) + list(range(GROUPZ - EDGE, GROUPZ))
+    bound = sorted({q // per for q in edge_planes}, reverse=True)
+    free = [o for o in range(last, -1, -1) if o not in bound]
+    far_side = jnp.where(low, 1, 0)
+
+    load.wait()
+    pl.semaphore_wait(barrier, n - 1 + jnp.where(has_below, 1, 0) + jnp.where(has_above, 1, 0))
+    near_side = 1 - far_side
+    far_free = [o for o in free if o >= n // 2]
+    far_bound = [o for o in bound if o >= n // 2]
+    near_free = [o for o in free if o < n // 2]
+    near_bound = [o for o in bound if o < n // 2]
+
+    for o in far_free:
+        blend_owner(mirrored(o))
+        send_owner(mirrored(o))
+    blend_edge(far_side)
+    send_edge(far_side)
+    for o in far_bound:
+        blend_owner(mirrored(o))
+        send_inner(o)
+    for o in near_free:
+        blend_owner(mirrored(o))
+        send_owner(mirrored(o))
+    for o in near_bound:
+        blend_owner(mirrored(o))
+        send_inner(o)
+    blend_edge(near_side)
 
     rec[...] = jnp.zeros_like(rec)
     for k in range(n):
@@ -204,7 +239,16 @@
             rec[j, s : s + frame] = rec[j, s : s + frame] + totals[j]
     rec[...] = 1.0 / jnp.maximum(rec[...], weight_floor)
 
+    wait_edge(far_side)
+    send_edge(near_side)
+    add_edge(far_side)
+    for o in far_bound:
+        send_bound(o)
     acc[...] = jnp.zeros_like(acc)
+    wait_edge(near_side)
+    add_edge(near_side)
+    for o in near_bound:
+        send_bound(o)
 
     def add(k, source):
         s = pl.multiple_of(frame_start(k), 8)
@@ -258,7 +302,7 @@
         dma = pltpu.SemaphoreType.DMA
         return pl.pallas_call(
             functools.partial(kernel, groups, n, per, depth, tile_rows, frame, acc_rows),
-            out_shape=jax.ShapeDtypeStruct((per, rows, cols), bf16),
+            out_shape=pltpu.VMEM((per, rows, cols), bf16),
             in_specs=[pl.BlockSpec(memory_space=pltpu.SMEM)] * 3
             + [pl.BlockSpec(memory_space=pltpu.VMEM), pl.BlockSpec(memory_space=pl.ANY)],
             out_specs=pl.BlockSpec(memory_space=pltpu.VMEM),

time: 25.3 us -> 20.2 us (0.80)
  the two profiles are of different devices: /device:TPU:29 before, /device:TPU:0 now
where the time goes in v2:
time: 20.2 us; the launch traced here: 20.1 us
  Pallas kernels  18.8 us (93%)
  local copies, waits for them, and re-layouts  1.31 us (6%)
    pallas_call x1, Pallas kernels, shards(): pl.pallas_call(functools.partial(kernel, groups, n, per, depth, tile_rows...  18.8 us
    pallas_call x1, local copies, waits for them, and re-layouts, shards(): pl.pallas_call(functools.partial(kernel, groups, n, per, depth, tile_rows...  1.31 us

profile of v2, /device:TPU:0, one launch (start us, length us, event | category | flops | bytes accessed | tf_op | source)
XLA Modules:
  0.0 20.1 jit_solution(10349051772071614932)
XLA Ops:
  0.0 18.8 %shard_map.55 = bf16[4,946,128]{2,1,0:T(8,128)(2,1)S(1)} custom-call(s32[2,32]{1,0:T(2,128)} %bitcast.3, s32[3,32]{1,0:T(4,128)} %bitcast.2, f32[68]{0:T(128)} %constant.4.clone.rampz, f32[296,128]{1,0:T(8,128)} %constant.5.clone.table, bf16[1,20,256,128]{3,2,1,0:T(8,128)(2,1)} %tile_ref.1), custom_call_target="tpu_custom_call" | custom-call | tf_op jit(solution)/shard_map/pallas_call | solution.py:303
  18.8 1.3 %copy.6 = bf16[4,946,128]{2,0,1:T(4,128)(2,1)} copy(bf16[4,946,128]{2,1,0:T(8,128)(2,1)S(1)} %shard_map.55) | data formatting | bytes 1937408 | tf_op jit(solution)/shard_map/pallas_call | solution.py:303

commit v3 on v2

--- a/solution.py
+++ b/solution.py
@@ -33,8 +33,8 @@
 
 def frame_start(rank):
     if isinstance(rank, int):
-        return max((rank * STEPY - JITY) // 8 * 8, 0)
-    return jnp.maximum((rank * STEPY + 8 - JITY) // 8 * 8 - 8, 0)
+        return max(rank * STEPY - JITY, 0)
+    return jnp.maximum(rank * STEPY - JITY, 0)
 
 
 def round_up(value, step):
@@ -43,9 +43,9 @@
 
 def kernel(
     groups, n, per, depth, tile_rows, frame, acc_rows,
-    offs, fracs, rampz, table, tile_ref, out_ref,
+    offs_ref, fracs_ref, rampz_ref, table_ref, tile_ref, out_ref,
     raw, coef, wa, wb, blend, edge_send, edge_recv, recv, acc, rec,
-    load_sem, es_sem, er_sem, s_sem, r_sem,
+    offs, fracs, rampz, table, small_sem, load_sem, es_sem, er_sem, s_sem, r_sem,
 ):
     g = lax.axis_index("slab")
     r = lax.axis_index("tile")
@@ -54,9 +54,6 @@
     cols = raw.shape[2]
     last = n - 1
 
-    load = pltpu.make_async_copy(tile_ref.at[0], raw.at[pl.ds(0, depth)], load_sem)
-    load.start()
-
     barrier = pltpu.get_barrier_semaphore()
     for i in range(1, n):
         pl.semaphore_signal(
@@ -73,12 +70,25 @@
     def _():
         pl.semaphore_signal(barrier, inc=1, device_id=(g + 1, r), device_id_type=MESH)
 
+    smalls = [
+        pltpu.make_async_copy(source, target, small_sem.at[i])
+        for i, (source, target) in enumerate(
+            [(offs_ref, offs), (fracs_ref, fracs), (rampz_ref, rampz), (table_ref, table)]
+        )
+    ]
+    for small in smalls:
+        small.start()
+    load = pltpu.make_async_copy(tile_ref.at[0], raw.at[pl.ds(0, depth)], load_sem)
+    load.start()
+
     def table_row(at):
         return jnp.clip(at, 0, table.shape[0] - frame)
 
     def rampz_at(z):
         return rampz[jnp.clip(z + PADZ, 0, rampz.shape[0] - 1)]
 
+    for small in smalls:
+        small.wait()
     corner = offs[0, me]
     shift = offs[1, me] - frame_start(r)
     fz = fracs[0, me].astype(jnp.float32) / QUANT
@@ -251,7 +261,7 @@
         send_bound(o)
 
     def add(k, source):
-        s = pl.multiple_of(frame_start(k), 8)
+        s = frame_start(k)
         for j in range(per):
             acc[j, pl.ds(s, frame)] = acc[j, pl.ds(s, frame)] + source[j].astype(jnp.float32)
 
@@ -291,7 +301,7 @@
         reach = max(
             min(k * STEPY + JITY, rows - tile_rows) + tile_rows - frame_start(k) for k in range(n)
         )
-        frame = round_up(reach, 16)
+        frame = round_up(reach, 8)
         acc_rows = round_up(max(rows, frame_start(n - 1) + frame), 16)
         plane = ramp(tile_rows, RY)[:, None] * ramp(cols, RX)[None, :]
         table = np.zeros((round_up(PADY + frame + 8, 8), cols), np.float32)
@@ -303,8 +313,7 @@
         return pl.pallas_call(
             functools.partial(kernel, groups, n, per, depth, tile_rows, frame, acc_rows),
             out_shape=pltpu.VMEM((per, rows, cols), bf16),
-            in_specs=[pl.BlockSpec(memory_space=pltpu.SMEM)] * 3
-            + [pl.BlockSpec(memory_space=pltpu.VMEM), pl.BlockSpec(memory_space=pl.ANY)],
+            in_specs=[pl.BlockSpec(memory_space=pl.ANY)] * 5,
             out_specs=pl.BlockSpec(memory_space=pltpu.VMEM),
             scratch_shapes=[
                 pltpu.VMEM((depth + 1, tile_rows, cols), bf16),
@@ -317,7 +326,11 @@
                 pltpu.VMEM((n, per, frame, cols), bf16),
                 pltpu.VMEM((per, acc_rows, cols), f32),
                 pltpu.VMEM((per, acc_rows, cols), f32),
-                dma, dma((2,)), dma((2,)), dma((n,)), dma((n,)),
+                pltpu.SMEM((offsets.shape[1], offsets.shape[0]), jnp.int32),
+                pltpu.SMEM((fracs.shape[1], fracs.shape[0]), jnp.int32),
+                pltpu.SMEM(rampz.shape, f32),
+                pltpu.VMEM(table.shape, f32),
+                dma((4,)), dma, dma((2,)), dma((2,)), dma((n,)), dma((n,)),
             ],
             compiler_params=pltpu.CompilerParams(collective_id=0, has_side_effects=True),
         )(offsets.T, fracs.T, jnp.asarray(rampz), jnp.asarray(table), tiles)

time: 20.2 us -> 19.1 us (0.946)
  Pallas kernels: 18.8 us -> 17.6 us
    pallas_call x1, Pallas kernels: 18.8 us -> 17.6 us  [shards(): pl.pallas_call(functools.partial(kernel, groups, n, per, depth, tile_rows...]
where the time goes in v3:
time: 19.1 us; the launch traced here: 18.9 us
  Pallas kernels  17.6 us (92%)
  local copies, waits for them, and re-layouts  1.31 us (7%)
    pallas_call x1, Pallas kernels, shards(): pl.pallas_call(functools.partial(kernel, groups, n, per, depth, tile_rows...  17.6 us
    pallas_call x1, local copies, waits for them, and re-layouts, shards(): pl.pallas_call(functools.partial(kernel, groups, n, per, depth, tile_rows...  1.31 us

profile of v3, /device:TPU:0, one launch (start us, length us, event | category | flops | bytes accessed | tf_op | source)
XLA Modules:
  0.0 18.9 jit_solution(5729016884186422527)
XLA Ops:
  0.0 17.6 %shard_map.55 = bf16[4,946,128]{2,1,0:T(8,128)(2,1)S(1)} custom-call(s32[2,32]{1,0:T(2,128)} %bitcast.3, s32[3,32]{1,0:T(4,128)} %bitcast.2, f32[68]{0:T(128)} %constant.4.clone.rampz_ref, f32[288,128]{1,0:T(8,128)} %constant.5.clone.table_ref, bf16[1,20,256,128]{3,2,1,0:T(8,128)(2,1)} %tile_ref.1), custom_call_target="tpu_custom_call" | custom-call | tf_op jit(solution)/shard_map/pallas_call | solution.py:313
  17.6 1.3 %copy.6 = bf16[4,946,128]{2,0,1:T(4,128)(2,1)} copy(bf16[4,946,128]{2,1,0:T(8,128)(2,1)S(1)} %shard_map.55) | data formatting | bytes 1937408 | tf_op jit(solution)/shard_map/pallas_call | solution.py:313

commit v4 on v3

--- a/solution.py
+++ b/solution.py
@@ -274,9 +274,9 @@
             device_id=(g, k), device_id_type=MESH,
         ).wait_recv()
         add(k, recv.at[k])
-    rows = out_ref.shape[1]
-    for j in range(per):
-        out_ref[j] = (acc[j, :rows] * rec[j, :rows]).astype(jnp.bfloat16)
+    rows = out_ref.shape[0]
+    joined = (acc[:, :rows] * rec[:, :rows]).astype(jnp.bfloat16)
+    out_ref[...] = jnp.swapaxes(joined, 0, 1)
 
     for i in range(1, n):
         k = lax.rem(r + i, n)
@@ -310,9 +310,9 @@
         rampz[PADZ : PADZ + depth] = ramp(depth, 2 * MARGIN)
         bf16, f32 = jnp.bfloat16, jnp.float32
         dma = pltpu.SemaphoreType.DMA
-        return pl.pallas_call(
+        joined = pl.pallas_call(
             functools.partial(kernel, groups, n, per, depth, tile_rows, frame, acc_rows),
-            out_shape=pltpu.VMEM((per, rows, cols), bf16),
+            out_shape=pltpu.VMEM((rows, per, cols), bf16),
             in_specs=[pl.BlockSpec(memory_space=pl.ANY)] * 5,
             out_specs=pl.BlockSpec(memory_space=pltpu.VMEM),
             scratch_shapes=[
@@ -334,6 +334,7 @@
             ],
             compiler_params=pltpu.CompilerParams(collective_id=0, has_side_effects=True),
         )(offsets.T, fracs.T, jnp.asarray(rampz), jnp.asarray(table), tiles)
+        return jnp.transpose(joined, (1, 0, 2))
 
     in_specs = (P(("slab", "tile"), None, None, None), P(), P())
     out_specs = P(("slab", "tile"), None, None)

time: 19.1 us -> 18.8 us (0.984)
  local copies, waits for them, and re-layouts: 1.31 us -> 0.94 us
    pallas_call x1 -> x0, local copies, waits for them, and re-layouts: 1.31 us -> none  [shards(): pl.pallas_call(functools.partial(kernel, groups, n, per, depth, tile_rows...]
    unnamed x0 -> x1, local copies, waits for them, and re-layouts: none -> 0.94 us
where the time goes in v4:
time: 18.8 us; the launch traced here: 18.6 us
  Pallas kernels  17.7 us (94%)
  local copies, waits for them, and re-layouts  0.94 us (5%)
    pallas_call x1, Pallas kernels, shards(): pl.pallas_call(functools.partial(kernel, groups, n, per, depth, tile_rows...  17.7 us
    unnamed x1, local copies, waits for them, and re-layouts  0.94 us

profile of v4, /device:TPU:0, one launch (start us, length us, event | category | flops | bytes accessed | tf_op | source)
XLA Modules:
  0.0 18.6 jit_solution(10704068812050694074)
XLA Ops:
  0.0 17.7 %shard_map.55 = bf16[946,4,128]{2,1,0:T(4,128)(2,1)S(1)} custom-call(s32[2,32]{1,0:T(2,128)} %bitcast.5, s32[3,32]{1,0:T(4,128)} %bitcast.4, f32[68]{0:T(128)} %constant.4.clone.rampz_ref, f32[288,128]{1,0:T(8,128)} %constant.5.clone.table_ref, bf16[1,20,256,128]{3,2,1,0:T(8,128)(2,1)} %tile_ref.1), custom_call_target="tpu_custom_call" | custom-call | tf_op jit(solution)/shard_map/pallas_call | solution.py:313
  17.7 0.9 %copy.7 = bf16[4,946,128]{2,0,1:T(4,128)(2,1)} copy(bf16[4,946,128]{2,0,1:T(4,128)(2,1)S(1)} %bitcast.3) | data formatting | bytes 1937408
